TPU v7x, 128 devices: a whole 4x4x4 slice. The times are simulated.
128 devices in a mesh: layer: 2 (over core), px: 16 (over x, z), py: 4 (over y).
Axes of the slice: x: 4, y: 4, z: 4, core: 2. Of those that a mesh axis runs over, the one named last changes fastest.
Arguments:
- right_side: float32 [8, 2048, 4096], P('layer', 'px', 'py'), may hold values from -30 to 30
- row_conduct: float32 [8, 2048, 4096], P('layer', 'px', 'py'), may hold values from 0.5 to 2
- column_conduct: float32 [8, 2048, 4096], P('layer', 'px', 'py'), may hold values from 0.5 to 2
- via_conduct: float32 [8, 2048, 4096], P('layer', 'px', 'py'), may hold values from 0.5 to 4
- via_mask: int32 [8, 2048, 4096], P('layer', 'px', 'py'), may hold values 0 or 1
- ground_conduct: float32 [8, 2048, 4096], P('layer', 'px', 'py'), may hold values from 0.01 to 0.1
Outputs:
- solution_field: float32 [8, 2048, 4096], P('layer', 'px', 'py')
- residual: float32 [8, 2048, 4096], P('layer', 'px', 'py')
All inputs are finite; a program needn't handle non-finite values. No bound on the sum of `via_mask` on one device may be relied on, other than what follows from the above.
Results may differ from a plain program's by a relative error of at most 0.0001.
Values sent between devices are 32-bit elements; how exact they have to be, the bound alone decides.
A program may use at most 128 MiB of HBM per device.

v0:
```python
import functools

import jax
import jax.numpy as jnp
from jax import lax
from jax.experimental import pallas as pl
from jax.experimental.pallas import tpu as pltpu
from jax.sharding import PartitionSpec as P

MESH = pl.DeviceIdType.MESH
S = 8
L = 128
F32 = jnp.float32


def kernel(sizes, chunks, b_hbm, r_hbm, c_hbm, via_hbm, mask_hbm, g_hbm, x_hbm, res_hbm,
           bb, rb, cb, ub, mb, gb, gain, inv, mid, ef, efo, f2, f2o, zb, zo, wb, vb, vo, ut,
           redge, cedge, chalo, fprev, colacc, row_s, row_r, col_s, col_r, red_s, red_r, sum_s, sum_r,
           load_sem, edge_sem, vm_sem, ef_sem, f2_sem, halo_sem, red_sem, sum_sem, out_sem):
    members, npx, npy = sizes
    depth, rows, width = bb.shape
    tiles = rows // S
    per = tiles // chunks
    last = depth - 1
    up = lax.axis_index("layer")
    px = lax.axis_index("px")
    py = lax.axis_index("py")
    lower = up == 0
    where_l = [k + up * (last - 2 * k) for k in range(depth)]
    where_u = [k + up * (last - 1 - 2 * k) for k in range(last)]
    chunk_rows = per * S

    edge_loads = [
        pltpu.make_async_copy(r_hbm.at[where_l[k], pl.ds(rows - S, S)], redge.at[k], edge_sem.at[0, k])
        for k in range(depth)
    ] + [
        pltpu.make_async_copy(c_hbm.at[where_l[k], :, pl.ds(width - L, L)], cedge.at[k], edge_sem.at[1, k])
        for k in range(depth)
    ]
    for copy in edge_loads:
        copy.start()
    top = [
        pltpu.make_async_copy(via_hbm.at[last], ub.at[last], load_sem.at[0, last]),
        pltpu.make_async_copy(mask_hbm.at[last], mb.at[last], load_sem.at[1, last]),
    ]

    @pl.when(lower)
    def _():
        for copy in top:
            copy.start()

    loads = []
    for k in range(last):
        loads.append(pltpu.make_async_copy(via_hbm.at[where_u[k]], ub.at[k], load_sem.at[0, k]))
        loads.append(pltpu.make_async_copy(mask_hbm.at[where_u[k]], mb.at[k], load_sem.at[1, k]))
    for k in range(depth):
        loads.append(pltpu.make_async_copy(r_hbm.at[where_l[k]], rb.at[k, pl.ds(S, rows)], load_sem.at[2, k]))
        loads.append(pltpu.make_async_copy(c_hbm.at[where_l[k]], cb.at[k], load_sem.at[3, k]))
        loads.append(pltpu.make_async_copy(g_hbm.at[where_l[k]], gb.at[k], load_sem.at[4, k]))
        loads.append(pltpu.make_async_copy(b_hbm.at[where_l[k]], bb.at[k], load_sem.at[5, k]))
    for copy in loads:
        copy.start()

    group = members * npy
    here = py * members + up

    def ring_peer(d):
        t = lax.rem(here + d, group)
        return (lax.rem(t, members), px, t // members)

    def px_peer(d):
        return (up, lax.rem(px + d, npx), py)

    row_r[...] = jnp.zeros_like(row_r)
    col_r[...] = jnp.zeros_like(col_r)
    barrier = pltpu.get_barrier_semaphore()
    for d in range(1, group):
        pl.semaphore_signal(barrier, inc=1, device_id=ring_peer(d), device_id_type=MESH)
    for d in range(1, npx):
        pl.semaphore_signal(barrier, inc=1, device_id=px_peer(d), device_id_type=MESH)

    lane = lax.broadcasted_iota(jnp.int32, (S, L), 1)
    sub = lax.broadcasted_iota(jnp.int32, (S, L), 0)
    sub_w = lax.broadcasted_iota(jnp.int32, (S, width), 0)
    lane_w = lax.broadcasted_iota(jnp.int32, (S, width), 1)

    partner = (1 - up, px, py)
    above, below = (up, px - 1, py), (up, px + 1, py)
    left, right = (up, px, py - 1), (up, px, py + 1)

    def remote(src, dst, sems, device):
        return pltpu.make_async_remote_copy(
            src_ref=src, dst_ref=dst, send_sem=sems.at[0], recv_sem=sems.at[1],
            device_id=device, device_id_type=MESH)

    def exchanges(trip):
        return (
            (px < npx - 1, px > 0, remote(row_s.at[trip, 0], row_r.at[trip, 0], halo_sem.at[trip, 0], below)),
            (px > 0, px < npx - 1, remote(row_s.at[trip, 1], row_r.at[trip, 1], halo_sem.at[trip, 1], above)),
            (py < npy - 1, py > 0, remote(col_s.at[trip, 0], col_r.at[trip, 0], halo_sem.at[trip, 2], right)),
            (py > 0, py < npy - 1, remote(col_s.at[trip, 1], col_r.at[trip, 1], halo_sem.at[trip, 3], left)),
        )

    def send_halo(trip, which):
        for e in which:
            sends, _, copy = exchanges(trip)[e]
            pl.when(sends)(copy.start)

    def take_halo(trip, which):
        for e in which:
            sends, takes, copy = exchanges(trip)[e]
            pl.when(takes)(copy.wait_recv)

    def end_halo(trip, which):
        for e in which:
            sends, _, copy = exchanges(trip)[e]
            pl.when(sends)(copy.wait_send)

    for copy in edge_loads:
        copy.wait()
    for k in range(depth):
        row_s[0, 0, k:k + 1, :] = redge[k, S - 1:S, :]
        acc = jnp.zeros((S, L), F32)
        for i in range(tiles):
            edge = jnp.broadcast_to(cedge[k, i * S:(i + 1) * S, L - 1:L], (S, L))
            acc += jnp.where(lane == sub + i * S, edge, 0.0)
        col_s[0, 0, k:k + 1, :] = jnp.sum(acc, axis=0, keepdims=True)
    pl.semaphore_wait(barrier, group - 1 + npx - 1)
    send_halo(0, (0, 2))

    vm_copy = remote(ub.at[last], ub.at[last], vm_sem, partner)

    @pl.when(lower)
    def _():
        for copy in top:
            copy.wait()

        def times(i, _):
            at = pl.ds(pl.multiple_of(i * S, S), S)
            ub[last, at, :] = ub[last, at, :] * mb[last, at, :].astype(F32)
            return 0

        lax.fori_loop(0, tiles, times, 0)
        vm_copy.start()

    for copy in loads:
        copy.wait()
    take_halo(0, (0, 2))
    for k in range(depth):
        rb[k, S - 1:S, :] = row_r[0, 0, k:k + 1, :]

    def column(ref, k, i):
        spread = jnp.broadcast_to(ref[k:k + 1, :], (S, L))
        return jnp.sum(jnp.where(lane == sub + i * S, spread, 0.0), axis=1, keepdims=True)

    def next_row(now, after):
        return pltpu.roll(jnp.where(sub_w == 0, after, now), S - 1, 0)

    def prev_row(now, before):
        return pltpu.roll(jnp.where(sub_w == S - 1, before, now), 1, 0)

    def rows_at(i):
        return pl.ds(pl.multiple_of(i * S, S), S)

    def factor_tile(i):
        at, pad = rows_at(i), rows_at(i + 1)
        coupling, g, y = None, None, None
        for k in range(depth):
            r = rb[k, pad, :]
            c = cb[k, at, :]
            edge = column(col_r.at[0, 0], k, i)
            chalo[k, at, :] = jnp.broadcast_to(edge, (S, L))
            c_left = jnp.where(lane_w == 0, edge, pltpu.roll(c, 1, 1))
            d = gb[k, at, :] + r + prev_row(r, rb[k, at, :]) + c + c_left
            rhs = bb[k, at, :]
            if k:
                d = d + coupling - coupling * g
                rhs = rhs + g * y
            y = rhs
            if k < last:
                coupling = ub[k, at, :] * mb[k, at, :].astype(F32)
                ub[k, at, :] = coupling
                inverse = 1.0 / (d + coupling)
                g = coupling * inverse
                gain[k, at, :] = g
                inv[k, at, :] = inverse
                zb[k, pad, :] = y * inverse
            else:
                ef[0, at, :] = d
                ef[1, at, :] = y

    def ef_copy(c):
        at = pl.ds(pl.multiple_of(c * chunk_rows, chunk_rows), chunk_rows)
        return remote(ef.at[:, at], efo.at[:, at], ef_sem.at[c], partner)

    def f2_copy(c):
        at = pl.ds(pl.multiple_of(c * chunk_rows, chunk_rows), chunk_rows)
        return remote(f2.at[at], f2o.at[at], f2_sem.at[c], partner)

    def in_chunks(tile, before=None, after=None):
        def chunk(c, _):
            if before is not None:
                before(c)

            def one(j, _):
                tile(c * per + j)
                return 0

            lax.fori_loop(0, per, one, 0)
            if after is not None:
                after(c)
            return 0

        lax.fori_loop(0, chunks, chunk, 0)

    in_chunks(factor_tile, after=lambda c: ef_copy(c).start())

    @pl.when(up == 1)
    def _():
        vm_copy.wait_recv()

    def collect(field, k, pad, i, value):
        field[k, pad, :] = value
        mine = lane == sub + i * S
        first = jnp.broadcast_to(value[:, 0:1], (S, L))
        final = jnp.broadcast_to(value[:, width - 1:width], (S, L))
        colacc[0, k] = jnp.where(mine, final, colacc[0, k])
        colacc[1, k] = jnp.where(mine, first, colacc[1, k])

    def back(field, other, i, own, own_other):
        at, pad = rows_at(i), rows_at(i + 1)
        other[at, :] = own_other
        value = own
        for k in range(last, -1, -1):
            if k < last:
                value = field[k, pad, :] + gain[k, at, :] * value
            collect(field, k, pad, i, value)

    def back_first(i):
        at = rows_at(i)
        e, f, eo, fo = ef[0, at, :], ef[1, at, :], efo[0, at, :], efo[1, at, :]
        vm = ub[last, at, :]
        shared = 1.0 / (e * eo + vm * (e + eo))
        own, cross, far = (eo + vm) * shared, vm * shared, (e + vm) * shared
        mid[0, at, :] = own
        mid[1, at, :] = cross
        mid[2, at, :] = far
        back(zb, zo, i, own * f + cross * fo, cross * f + far * fo)

    def back_second(i):
        at = rows_at(i)
        f, fo = f2[at, :], f2o[at, :]
        own, cross, far = mid[0, at, :], mid[1, at, :], mid[2, at, :]
        back(vb, vo, i, own * f + cross * fo, cross * f + far * fo)

    def exchange(field, trip):
        for k in range(depth):
            row_s[trip, 0, k:k + 1, :] = field[k, rows + S - 1:rows + S, :]
            row_s[trip, 1, k:k + 1, :] = field[k, S:S + 1, :]
            for side in range(2):
                col_s[trip, side, k:k + 1, :] = jnp.sum(colacc[side, k], axis=0, keepdims=True)
        send_halo(trip, range(4))

    def receive(field, trip):
        take_halo(trip, range(4))
        for k in range(depth):
            field[k, S - 1:S, :] = row_r[trip, 0, k:k + 1, :]
            field[k, rows + S:rows + S + 1, :] = row_r[trip, 1, k:k + 1, :]
            now = field[k, 0:S, :]
            fprev[k] = rb[k, 0:S, :] * (now - next_row(now, field[k, S:2 * S, :]))

    def operate(field, other, trip, i):
        at, pad, ahead = rows_at(i), rows_at(i + 1), rows_at(i + 2)
        images, values = [], []
        carried = None
        value = field[0, pad, :]
        for k in range(depth):
            follow = field[k + 1, pad, :] if k < last else other[at, :]
            flow = rb[k, pad, :] * (value - next_row(value, field[k, ahead, :]))
            image = gb[k, at, :] * value + flow - prev_row(flow, fprev[k])
            fprev[k] = flow
            before = column(col_r.at[trip, 0], k, i)
            after = column(col_r.at[trip, 1], k, i)
            beside = jnp.where(lane_w == width - 1, after, pltpu.roll(value, width - 1, 1))
            flow = cb[k, at, :] * (value - beside)
            into = chalo[k, at, 0:1] * (before - value[:, 0:1])
            image = image + flow - jnp.where(lane_w == 0, into, pltpu.roll(flow, 1, 1))
            flow = ub[k, at, :] * (value - follow)
            image = image + flow
            if k:
                image = image - carried
            carried = flow
            images.append(image)
            values.append(value)
            value = follow
        return images, values

    def fold(product):
        total = product[:, 0:L]
        for j in range(1, width // L):
            total = total + product[:, j * L:(j + 1) * L]
        return total

    def sum_copies(slot):
        return [
            remote(red_s.at[slot], red_r.at[slot, d], red_sem.at[slot, d], ring_peer(d)) for d in range(1, group)
        ], [
            remote(sum_s.at[slot], sum_r.at[slot, d], sum_sem.at[slot, d], px_peer(d)) for d in range(1, npx)
        ]

    def sum_begin(slot, one, two):
        red_s[slot, 0:1, :] = jnp.sum(one, axis=0, keepdims=True)
        red_s[slot, 1:2, :] = jnp.sum(two, axis=0, keepdims=True)
        for copy in sum_copies(slot)[0]:
            copy.start()

    def sum_middle(slot):
        total = red_s[slot]
        for d, copy in enumerate(sum_copies(slot)[0]):
            copy.wait_recv()
            total = total + red_r[slot, d + 1]
        sum_s[slot] = total
        for copy in sum_copies(slot)[1]:
            copy.start()

    def sum_finish(slot):
        total = sum_s[slot]
        for d, copy in enumerate(sum_copies(slot)[1]):
            copy.wait_recv()
            total = total + sum_r[slot, d + 1]
        total = jnp.sum(total, axis=1, keepdims=True)
        return total[0:1], total[1:2]

    def sum_end(slot):
        for copies in sum_copies(slot):
            for copy in copies:
                copy.wait_send()

    colacc[...] = jnp.zeros_like(colacc)
    in_chunks(back_first, before=lambda c: ef_copy(c).wait_recv())
    exchange(zb, 1)
    receive(zb, 1)

    zero = jnp.zeros((S, L), F32)

    def image_first(i, sums):
        at, pad = rows_at(i), rows_at(i + 1)
        images, values = operate(zb, zo, 1, i)
        one, two = sums
        y = None
        for k in range(depth):
            wb[k, at, :] = images[k]
            one = one + fold(bb[k, at, :] * values[k])
            two = two + fold(images[k] * values[k])
            y = images[k] if k == 0 else images[k] + gain[k - 1, at, :] * y
            if k < last:
                vb[k, pad, :] = y * inv[k, at, :]
            else:
                f2[at, :] = y
        return one, two

    def first_chunk(c, sums):
        sums = lax.fori_loop(0, per, lambda j, s: image_first(c * per + j, s), sums)
        f2_copy(c).start()
        return sums

    one, two = lax.fori_loop(0, chunks, first_chunk, (zero, zero))
    sum_begin(0, one, two)
    in_chunks(back_second, before=lambda c: f2_copy(c).wait_recv())
    exchange(vb, 2)
    sum_middle(0)
    receive(vb, 2)
    rho, power = sum_finish(0)
    alpha = rho / power

    def image_second(i, sums):
        at, pad = rows_at(i), rows_at(i + 1)
        images, values = operate(vb, vo, 2, i)
        one, two = sums
        for k in range(depth):
            ut[k, at, :] = images[k]
            w = wb[k, at, :]
            precond = zb[k, pad, :] - alpha * values[k]
            one = one + fold((bb[k, at, :] - alpha * w) * precond)
            two = two + fold((w - alpha * images[k]) * precond)
        return one, two

    one, two = lax.fori_loop(0, tiles, image_second, (zero, zero))
    sum_begin(1, one, two)
    sum_middle(1)
    rho_next, curvature = sum_finish(1)
    ratio = rho_next / rho
    beta = rho_next / (curvature - ratio * rho_next / alpha)
    on_z = alpha + beta * (1.0 + ratio)
    on_v = beta * alpha

    def finish(i, _):
        at, pad = rows_at(i), rows_at(i + 1)
        for k in range(depth):
            gb[k, at, :] = on_z * zb[k, pad, :] - on_v * vb[k, pad, :]
            cb[k, at, :] = bb[k, at, :] - on_z * wb[k, at, :] + on_v * ut[k, at, :]
        return 0

    outs = []

    def out_copies(c):
        at = pl.ds(pl.multiple_of(c * chunk_rows, chunk_rows), chunk_rows)
        return [
            pltpu.make_async_copy(gb.at[k, at], x_hbm.at[where_l[k], at], out_sem.at[0, k, c]) for k in range(depth)
        ] + [
            pltpu.make_async_copy(cb.at[k, at], res_hbm.at[where_l[k], at], out_sem.at[1, k, c]) for k in range(depth)
        ]

    def finish_chunk(c, _):
        lax.fori_loop(0, per, lambda j, s: finish(c * per + j, s), 0)
        for copy in out_copies(c):
            copy.start()
        return 0

    lax.fori_loop(0, chunks, finish_chunk, 0)

    end_halo(0, (0, 2))
    end_halo(1, range(4))
    end_halo(2, range(4))

    @pl.when(lower)
    def _():
        vm_copy.wait_send()

    def close(c, _):
        ef_copy(c).wait_send()
        f2_copy(c).wait_send()
        for copy in out_copies(c):
            copy.wait()
        return 0

    lax.fori_loop(0, chunks, close, 0)
    sum_end(0)
    sum_end(1)


def solution(mesh):
    sizes = tuple(mesh.shape[name] for name in ("layer", "px", "py"))
    members, npx, npy = sizes
    assert members == 2

    def shards(*arrays):
        depth, rows, width = arrays[0].shape
        assert rows <= L and rows % S == 0 and width % L == 0 and depth >= 2
        chunks = max(c for c in (1, 2, 4) if (rows // S) % c == 0)
        group = members * npy
        full, plane = (depth, rows, width), (rows, width)
        padded = (depth, rows + 2 * S, width)
        dma = pltpu.SemaphoreType.DMA

        def vmem(*shape, dtype=F32):
            return pltpu.VMEM(shape, dtype)

        scratch = [
            vmem(*full), vmem(depth, rows + S, width), vmem(*full), vmem(*full), vmem(*full, dtype=jnp.int32),
            vmem(*full), vmem(depth - 1, *plane), vmem(depth - 1, *plane), vmem(3, *plane), vmem(2, *plane),
            vmem(2, *plane), vmem(*plane), vmem(*plane), vmem(*padded), vmem(*plane), vmem(*full), vmem(*padded),
            vmem(*plane), vmem(*full),
            vmem(depth, S, width), vmem(depth, rows, L), vmem(depth, rows, L), vmem(depth, S, width),
            vmem(2, depth, S, L),
            vmem(3, 2, depth, width), vmem(3, 2, depth, width), vmem(3, 2, depth, L), vmem(3, 2, depth, L),
            vmem(2, 2, L), vmem(2, group, 2, L), vmem(2, 2, L), vmem(2, npx, 2, L),
            dma((6, depth)), dma((2, depth)), dma((2,)), dma((chunks, 2)), dma((chunks, 2)), dma((3, 4, 2)),
            dma((2, group, 2)), dma((2, npx, 2)), dma((2, depth, chunks)),
        ]
        return pl.pallas_call(
            functools.partial(kernel, sizes, chunks),
            out_shape=(jax.ShapeDtypeStruct(full, F32), jax.ShapeDtypeStruct(full, F32)),
            in_specs=[pl.BlockSpec(memory_space=pl.ANY)] * 6,
            out_specs=(pl.BlockSpec(memory_space=pl.ANY),) * 2,
            scratch_shapes=scratch,
            compiler_params=pltpu.CompilerParams(collective_id=0, has_side_effects=True),
            name="pcg",
        )(*arrays)

    spec = P("layer", "px", "py")
    return jax.shard_map(shards, mesh=mesh, in_specs=(spec,) * 6, out_specs=(spec, spec), check_vma=False)
```

profile of v0, /device:TPU:1, one launch (start us, length us, event | category | flops | bytes accessed | tf_op | source)
XLA Modules:
  0.0 54.6 jit_solution(8504280121380030193)
XLA Ops:
  0.6 49.3 %pcg.1 = (f32[4,128,1024]{2,1,0:T(8,128)}, f32[4,128,1024]{2,1,0:T(8,128)}) custom-call(f32[4,128,1024]{2,1,0:T(8,128)} %b_hbm.1, f32[4,128,1024]{2,1,0:T(8,128)} %r_hbm.1, f32[4,128,1024]{2,1,0:T(8,128)} %c_hbm.1, f32[4,128,1024]{2,1,0:T(8,128)} %via_hbm.1, s32[4,128,1024]{2,1,0:T(8,128)} %mask_hbm.1, f32[4,128,1024]{2,1,0:T(8,128)} %g_hbm.1), custom_call_target="tpu_custom_call" | custom-call | tf_op jit(solution)/shard_map/pcg/pallas_call | solution.py:471
  49.9 0.0 copy-start
  49.9 3.3 %copy.10 = f32[4,128,1024]{2,1,0:T(8,128)} copy(f32[4,128,1024]{2,1,0:T(8,128)} %get-tuple-element.4) | data formatting | bytes 4194304
  53.2 0.0 copy-done
  53.2 1.3 %copy.11 = f32[4,128,1024]{2,1,0:T(8,128)} copy(f32[4,128,1024]{2,1,0:T(8,128)S(1)} %copy-done) | data formatting | bytes 4194304
Async XLA Ops:
  49.9 3.3 %copy-start = (f32[4,128,1024]{2,1,0:T(8,128)S(1)}, f32[4,128,1024]{2,1,0:T(8,128)}, u32[]{:S(2)}) copy-start(f32[4,128,1024]{2,1,0:T(8,128)} %get-tuple-element.5) | copy-start | bytes 6291460
where the time goes:
time: 54.7 us; the launch traced here: 54.6 us
  Pallas kernels  49.3 us (90%)
  local copies, waits for them, and re-layouts  4.63 us (8%)
  between operations  0.65 us (1%)
    pallas_call x1, Pallas kernels, shards(): pl.pallas_call(functools.partial(kernel, sizes, chunks), out_shape=(jax.S...  49.3 us
    unnamed x4, local copies, waits for them, and re-layouts  4.63 us

commit v1 on v0

v1 whole, which is shorter than its diff:
```python
import functools

import jax
import jax.numpy as jnp
from jax import lax
from jax.experimental import pallas as pl
from jax.experimental.pallas import tpu as pltpu
from jax.sharding import PartitionSpec as P

MESH = pl.DeviceIdType.MESH
S = 8
L = 128
F32 = jnp.float32


def kernel(sizes, chunks, b_hbm, r_hbm, c_hbm, via_hbm, mask_hbm, g_hbm, bb, zb, vb, wb, ut, coef,
           rb, cb, ub, mb, gb, vm, vmask, gain, inv, mid, ef, efo, f2, f2o,
           redge, cedge, pprev, colacc, row_s, row_r, col_s, col_r, red_s, red_r, sum_s, sum_r,
           load_sem, edge_sem, top_sem, vm_sem, ef_sem, f2_sem, halo_sem, red_sem, sum_sem):
    members, npx, npy = sizes
    depth, rows, width = bb.shape
    tiles = rows // S
    per = tiles // chunks
    last = depth - 1
    blocks = width // L
    up = lax.axis_index("layer")
    px = lax.axis_index("px")
    py = lax.axis_index("py")
    lower = up == 0
    lay = [k + up * (last - 2 * k) for k in range(depth)]
    via_at = [k + up * (last - 1 - 2 * k) for k in range(last)]
    chunk_rows = per * S
    peers = npx * npy
    me = px * npy + py

    partner = (1 - up, px, py)
    above, below = (up, px - 1, py), (up, px + 1, py)
    left, right = (up, px, py - 1), (up, px, py + 1)

    def peer(d):
        t = lax.rem(me + d, peers)
        return (up, t // npy, lax.rem(t, npy))

    row_r[...] = jnp.zeros_like(row_r)
    col_r[...] = jnp.zeros_like(col_r)
    barrier = pltpu.get_barrier_semaphore()
    pl.semaphore_signal(barrier, inc=1, device_id=partner, device_id_type=MESH)

    def greet(d, _):
        pl.semaphore_signal(barrier, inc=1, device_id=peer(d), device_id_type=MESH)
        return 0

    edge_loads = [
        pltpu.make_async_copy(r_hbm.at[:, pl.ds(rows - S, S)], redge, edge_sem.at[0]),
        pltpu.make_async_copy(c_hbm.at[:, :, pl.ds(width - L, L)], cedge, edge_sem.at[1]),
    ]
    for copy in edge_loads:
        copy.start()
    top = [
        pltpu.make_async_copy(via_hbm.at[last], vm, top_sem.at[0]),
        pltpu.make_async_copy(mask_hbm.at[last], vmask, top_sem.at[1]),
    ]

    @pl.when(lower)
    def _():
        for copy in top:
            copy.start()

    def loads(c):
        start = pl.multiple_of(c * chunk_rows, chunk_rows)
        at = pl.ds(start, chunk_rows)
        pad = pl.ds(pl.multiple_of(start + S, S), chunk_rows)
        inner = pl.ds(0, last)
        pairs = [(via_hbm.at[inner, at], ub.at[:, at]), (mask_hbm.at[inner, at], mb.at[:, at]),
                 (r_hbm.at[:, at], rb.at[:, pad]), (c_hbm.at[:, at], cb.at[:, at]),
                 (g_hbm.at[:, at], gb.at[:, at]), (b_hbm.at[:, at], bb.at[:, at])]
        return [pltpu.make_async_copy(src, dst, load_sem.at[a, c]) for a, (src, dst) in enumerate(pairs)]

    for c in range(chunks):
        for copy in loads(c):
            copy.start()

    lax.fori_loop(1, peers, greet, 0)

    lane = lax.broadcasted_iota(jnp.int32, (S, L), 1)
    sub = lax.broadcasted_iota(jnp.int32, (S, L), 0)
    first_lane, final_lane = lane == 0, lane == L - 1
    first_sub, final_sub = sub == 0, sub == S - 1

    def remote(src, dst, sems, device):
        return pltpu.make_async_remote_copy(
            src_ref=src, dst_ref=dst, send_sem=sems.at[0], recv_sem=sems.at[1],
            device_id=device, device_id_type=MESH)

    def exchanges(trip):
        return (
            (px < npx - 1, px > 0, remote(row_s.at[trip, 0], row_r.at[trip, 0], halo_sem.at[trip, 0], below)),
            (px > 0, px < npx - 1, remote(row_s.at[trip, 1], row_r.at[trip, 1], halo_sem.at[trip, 1], above)),
            (py < npy - 1, py > 0, remote(col_s.at[trip, 0], col_r.at[trip, 0], halo_sem.at[trip, 2], right)),
            (py > 0, py < npy - 1, remote(col_s.at[trip, 1], col_r.at[trip, 1], halo_sem.at[trip, 3], left)),
        )

    def send_halo(trip, which):
        for e in which:
            sends, _, copy = exchanges(trip)[e]
            pl.when(sends)(copy.start)

    def take_halo(trip, which):
        for e in which:
            sends, takes, copy = exchanges(trip)[e]
            pl.when(takes)(copy.wait_recv)

    def end_halo(trip, which):
        for e in which:
            sends, _, copy = exchanges(trip)[e]
            pl.when(sends)(copy.wait_send)

    for copy in edge_loads:
        copy.wait()
    for k in range(depth):
        row_s[0, 0, k:k + 1, :] = redge[lay[k], S - 1:S, :]
        acc = jnp.zeros((S, L), F32)
        for i in range(tiles):
            edge = jnp.broadcast_to(cedge[lay[k], i * S:(i + 1) * S, L - 1:L], (S, L))
            acc = jnp.where(lane == sub + i * S, edge, acc)
        col_s[0, 0, k:k + 1, :] = jnp.sum(acc, axis=0, keepdims=True)

    vm_copy = remote(vm, vm, vm_sem, partner)

    @pl.when(lower)
    def _():
        for copy in top:
            copy.wait()

        def times(i, _):
            at = pl.ds(pl.multiple_of(i * S, S), S)
            vm[at, :] = vm[at, :] * vmask[at, :].astype(F32)
            return 0

        lax.fori_loop(0, tiles, times, 0)

    pl.semaphore_wait(barrier, peers)
    send_halo(0, (0, 2))
    pl.when(lower)(vm_copy.start)

    take_halo(0, (0, 2))
    for k in range(depth):
        rb[lay[k], S - 1:S, :] = row_r[0, 0, k:k + 1, :]

    def column(ref, k, i):
        spread = jnp.broadcast_to(ref[k:k + 1, :], (S, L))
        return jnp.sum(jnp.where(lane == sub + i * S, spread, 0.0), axis=1, keepdims=True)

    def rows_at(i):
        return pl.ds(pl.multiple_of(i * S, S), S)

    def cut(j):
        return pl.ds(j * L, L)

    def next_row(now, after):
        return pltpu.roll(jnp.where(first_sub, after, now), S - 1, 0)

    def prev_row(now, before):
        return pltpu.roll(jnp.where(final_sub, before, now), 1, 0)

    def from_left(parts, edge):
        turned = [pltpu.roll(p, 1, 1) for p in parts]
        return [jnp.where(first_lane, turned[j - 1] if j else edge, turned[j]) for j in range(blocks)]

    def from_right(parts, edge):
        turned = [pltpu.roll(p, L - 1, 1) for p in parts]
        return [jnp.where(final_lane, turned[j + 1] if j < blocks - 1 else edge, turned[j]) for j in range(blocks)]

    def factor_tile(i):
        at, pad = rows_at(i), rows_at(i + 1)
        coupling, g, y = [None] * blocks, [None] * blocks, [None] * blocks
        for k in range(depth):
            edge = column(col_r.at[0, 0], k, i)
            c = [cb[lay[k], at, cut(j)] for j in range(blocks)]
            c_left = from_left(c, edge)
            for j in range(blocks):
                r = rb[lay[k], pad, cut(j)]
                d = gb[lay[k], at, cut(j)] + r + prev_row(r, rb[lay[k], at, cut(j)]) + c[j] + c_left[j]
                rhs = bb[lay[k], at, cut(j)]
                if k:
                    d = d + coupling[j] - coupling[j] * g[j]
                    rhs = rhs + g[j] * y[j]
                y[j] = rhs
                if k < last:
                    coupling[j] = ub[via_at[k], at, cut(j)] * mb[via_at[k], at, cut(j)].astype(F32)
                    inverse = 1.0 / (d + coupling[j])
                    g[j] = coupling[j] * inverse
                    gain[k, at, cut(j)] = g[j]
                    inv[k, at, cut(j)] = inverse
                    zb[lay[k], pad, cut(j)] = rhs * inverse
                else:
                    ef[0, at, cut(j)] = d
                    ef[1, at, cut(j)] = rhs

    def chunk_at(c):
        return pl.ds(pl.multiple_of(c * chunk_rows, chunk_rows), chunk_rows)

    def ef_copy(c):
        return remote(ef.at[:, chunk_at(c)], efo.at[:, chunk_at(c)], ef_sem.at[c], partner)

    def f2_copy(c):
        return remote(f2.at[chunk_at(c)], f2o.at[chunk_at(c)], f2_sem.at[c], partner)

    def in_chunks(tile, before=None, after=None):
        def chunk(c, _):
            if before is not None:
                before(c)

            def one(j, _):
                tile(c * per + j)
                return 0

            lax.fori_loop(0, per, one, 0)
            if after is not None:
                after(c)
            return 0

        lax.fori_loop(0, chunks, chunk, 0)

    def wait_loads(c):
        for copy in loads(c):
            copy.wait()

    in_chunks(factor_tile, before=wait_loads, after=lambda c: ef_copy(c).start())

    @pl.when(up == 1)
    def _():
        vm_copy.wait_recv()

    def back(field, i, own):
        at, pad = rows_at(i), rows_at(i + 1)
        mine = lane == sub + i * S
        value = own
        for k in range(last, -1, -1):
            for j in range(blocks):
                if k < last:
                    value[j] = field[lay[k], pad, cut(j)] + gain[k, at, cut(j)] * value[j]
                field[lay[k], pad, cut(j)] = value[j]
            first = jnp.broadcast_to(value[0][:, 0:1], (S, L))
            final = jnp.broadcast_to(value[blocks - 1][:, L - 1:L], (S, L))
            colacc[0, k] = jnp.where(mine, final, colacc[0, k])
            colacc[1, k] = jnp.where(mine, first, colacc[1, k])

    def back_first(i):
        at = rows_at(i)
        value = []
        for j in range(blocks):
            e, f = ef[0, at, cut(j)], ef[1, at, cut(j)]
            eo, fo = efo[0, at, cut(j)], efo[1, at, cut(j)]
            v = vm[at, cut(j)]
            shared = 1.0 / (e * eo + v * (e + eo))
            own, cross = (eo + v) * shared, v * shared
            mid[0, at, cut(j)] = own
            mid[1, at, cut(j)] = cross
            value.append(own * f + cross * fo)
        back(zb, i, value)

    def back_second(i):
        at = rows_at(i)
        back(vb, i, [mid[0, at, cut(j)] * f2[at, cut(j)] + mid[1, at, cut(j)] * f2o[at, cut(j)] for j in range(blocks)])

    def exchange(field, trip):
        for k in range(depth):
            row_s[trip, 0, k:k + 1, :] = field[lay[k], rows + S - 1:rows + S, :]
            row_s[trip, 1, k:k + 1, :] = field[lay[k], S:S + 1, :]
            final = jnp.sum(colacc[0, k], axis=0, keepdims=True)
            col_s[trip, 0, k:k + 1, :] = final * col_s[0, 0, k:k + 1, :]
            col_s[trip, 1, k:k + 1, :] = jnp.sum(colacc[1, k], axis=0, keepdims=True)
        send_halo(trip, range(4))

    def receive(field, trip):
        take_halo(trip, range(4))
        for k in range(depth):
            field[lay[k], S - 1:S, :] = row_r[trip, 0, k:k + 1, :]
            field[lay[k], rows + S:rows + S + 1, :] = row_r[trip, 1, k:k + 1, :]
            for j in range(blocks):
                pprev[k, :, cut(j)] = rb[lay[k], 0:S, cut(j)] * field[lay[k], 0:S, cut(j)]

    def sideways(field, trip, i, k):
        at, pad, ahead = rows_at(i), rows_at(i + 1), rows_at(i + 2)
        value = [field[lay[k], pad, cut(j)] for j in range(blocks)]
        c = [cb[lay[k], at, cut(j)] for j in range(blocks)]
        before = column(col_r.at[trip, 0], k, i)
        after = column(col_r.at[trip, 1], k, i)
        to_right = from_left([c[j] * value[j] for j in range(blocks)], before)
        beside = from_right(value, after)
        out = []
        for j in range(blocks):
            r = rb[lay[k], pad, cut(j)]
            down = r * value[j]
            term = r * next_row(value[j], field[lay[k], ahead, cut(j)]) + prev_row(down, pprev[k, :, cut(j)])
            pprev[k, :, cut(j)] = down
            out.append(term + (c[j] * beside[j] + to_right[j]))
        return out, value

    def pack(one, two):
        one = jnp.sum(one, axis=0, keepdims=True)
        two = jnp.sum(two, axis=0, keepdims=True)
        one = one + pltpu.roll(one, L // 2, 1)
        two = two + pltpu.roll(two, L // 2, 1)
        return jnp.where(lane[0:1] < L // 2, one, two)

    def red_copy(slot):
        return remote(red_s.at[slot], red_r.at[slot], red_sem.at[slot], partner)

    def sum_begin(slot, one, two):
        red_s[slot] = pack(one, two)
        red_copy(slot).start()

    def sum_copy(slot, d):
        return remote(sum_s.at[slot], sum_r.at[slot, me], sum_sem.at[slot], peer(d))

    def sum_middle(slot):
        red_copy(slot).wait_recv()
        total = red_s[slot] + red_r[slot]
        sum_s[slot] = total
        sum_r[slot, me] = total

        def send(d, _):
            sum_copy(slot, d).start()
            return 0

        lax.fori_loop(1, peers, send, 0)

    def sum_bytes(slot, side):
        part = sum_r.at[slot, pl.ds(0, peers - 1)]
        return pltpu.make_async_copy(part, part, sum_sem.at[slot, side])

    def sum_finish(slot):
        sum_bytes(slot, 1).wait()
        total = jnp.sum(sum_r[slot], axis=0)
        low = jnp.sum(jnp.where(lane[0:1] < L // 2, total, 0.0), axis=1, keepdims=True)
        high = jnp.sum(jnp.where(lane[0:1] < L // 2, 0.0, total), axis=1, keepdims=True)
        return low, high

    def sum_end(slot):
        red_copy(slot).wait_send()
        sum_bytes(slot, 0).wait()

    colacc[...] = jnp.zeros_like(colacc)
    in_chunks(back_first, before=lambda c: ef_copy(c).wait_recv())
    exchange(zb, 1)
    receive(zb, 1)

    zero = jnp.zeros((S, L), F32)

    def image_first(i, sums):
        at, pad = rows_at(i), rows_at(i + 1)
        one, two = sums
        y = [None] * blocks
        for k in range(depth):
            near, value = sideways(zb, 1, i, k)
            for j in range(blocks):
                b = bb[lay[k], at, cut(j)]
                w = b - near[j]
                wb[lay[k], at, cut(j)] = w
                one = one + b * value[j]
                two = two + w * value[j]
                y[j] = w if k == 0 else w + gain[k - 1, at, cut(j)] * y[j]
                if k < last:
                    vb[lay[k], pad, cut(j)] = y[j] * inv[k, at, cut(j)]
                else:
                    f2[at, cut(j)] = y[j]
        return one, two

    def first_chunk(c, sums):
        sums = lax.fori_loop(0, per, lambda j, s: image_first(c * per + j, s), sums)
        f2_copy(c).start()
        return sums

    one, two = lax.fori_loop(0, chunks, first_chunk, (zero, zero))
    sum_begin(0, one, two)
    in_chunks(back_second, before=lambda c: f2_copy(c).wait_recv())
    exchange(vb, 2)
    sum_middle(0)
    receive(vb, 2)
    rho, power = sum_finish(0)
    alpha = rho / power
    step = jnp.broadcast_to(alpha, (S, L))

    def image_second(i, sums):
        at, pad = rows_at(i), rows_at(i + 1)
        one, two = sums
        for k in range(depth):
            near, value = sideways(vb, 2, i, k)
            for j in range(blocks):
                w = wb[lay[k], at, cut(j)]
                u = w - near[j]
                ut[lay[k], at, cut(j)] = u
                precond = zb[lay[k], pad, cut(j)] - step * value[j]
                one = one + (bb[lay[k], at, cut(j)] - step * w) * precond
                two = two + (w - step * u) * precond
        return one, two

    one, two = lax.fori_loop(0, tiles, image_second, (zero, zero))
    sum_begin(1, one, two)
    sum_middle(1)
    rho_next, curvature = sum_finish(1)
    ratio = rho_next / rho
    beta = rho_next / (curvature - ratio * rho_next / alpha)
    coef[0] = jnp.broadcast_to(alpha + beta * (1.0 + ratio), (S, L))
    coef[1] = jnp.broadcast_to(beta * alpha, (S, L))

    end_halo(0, (0, 2))
    end_halo(1, range(4))
    end_halo(2, range(4))
    pl.when(lower)(vm_copy.wait_send)

    def close(c, _):
        ef_copy(c).wait_send()
        f2_copy(c).wait_send()
        return 0

    lax.fori_loop(0, chunks, close, 0)
    sum_end(0)
    sum_end(1)


def finish(chunks, bb, zb, vb, wb, ut, coef, x_hbm, res_hbm, xb, resb, out_sem):
    depth, rows, width = bb.shape
    chunk_rows = rows // chunks
    on_z, on_v = coef[0], coef[1]

    def out_copies(c):
        at = pl.ds(c * chunk_rows, chunk_rows)
        return [pltpu.make_async_copy(xb.at[:, at], x_hbm.at[:, at], out_sem.at[0, c]),
                pltpu.make_async_copy(resb.at[:, at], res_hbm.at[:, at], out_sem.at[1, c])]

    for c in range(chunks):
        def tile(t, _):
            start = pl.multiple_of(c * chunk_rows + t * S, S)
            at, pad = pl.ds(start, S), pl.ds(pl.multiple_of(start + S, S), S)
            for k in range(depth):
                for j in range(width // L):
                    cut = pl.ds(j * L, L)
                    xb[k, at, cut] = on_z * zb[k, pad, cut] - on_v * vb[k, pad, cut]
                    resb[k, at, cut] = bb[k, at, cut] - on_z * wb[k, at, cut] + on_v * ut[k, at, cut]
            return 0

        lax.fori_loop(0, chunk_rows // S, tile, 0)
        for copy in out_copies(c):
            copy.start()
    for c in range(chunks):
        for copy in out_copies(c):
            copy.wait()


def solution(mesh):
    sizes = tuple(mesh.shape[name] for name in ("layer", "px", "py"))
    members, npx, npy = sizes
    assert members == 2

    def shards(*arrays):
        depth, rows, width = arrays[0].shape
        assert rows <= L and rows % S == 0 and width % L == 0 and depth >= 2
        chunks = max(c for c in (1, 2, 4) if (rows // S) % c == 0)
        peers = npx * npy
        full, plane, inner = (depth, rows, width), (rows, width), (depth - 1, rows, width)
        padded = (depth, rows + 2 * S, width)
        dma = pltpu.SemaphoreType.DMA

        def vmem(*shape, dtype=F32):
            return pltpu.VMEM(shape, dtype)

        scratch = [
            vmem(depth, rows + S, width), vmem(*full), vmem(*inner), vmem(*inner, dtype=jnp.int32), vmem(*full),
            vmem(*plane), vmem(*plane, dtype=jnp.int32),
            vmem(*inner), vmem(*inner), vmem(2, *plane), vmem(2, *plane), vmem(2, *plane), vmem(*plane), vmem(*plane),
            vmem(depth, S, width), vmem(depth, rows, L), vmem(depth, S, width), vmem(2, depth, S, L),
            vmem(3, 2, depth, width), vmem(3, 2, depth, width), vmem(3, 2, depth, L), vmem(3, 2, depth, L),
            vmem(2, 1, L), vmem(2, 1, L), vmem(2, 1, L), vmem(2, peers, 1, L),
            dma((6, chunks)), dma((2,)), dma((2,)), dma((2,)), dma((chunks, 2)), dma((chunks, 2)), dma((3, 4, 2)),
            dma((2, 2)), dma((2, 2)),
        ]
        anywhere = pl.BlockSpec(memory_space=pl.ANY)
        kept = pl.pallas_call(
            functools.partial(kernel, sizes, chunks),
            out_shape=(vmem(*full), vmem(*padded), vmem(*padded), vmem(*full), vmem(*full), vmem(2, S, L)),
            in_specs=[anywhere] * 6,
            out_specs=(pl.BlockSpec(memory_space=pltpu.VMEM),) * 6,
            scratch_shapes=scratch,
            compiler_params=pltpu.CompilerParams(
                collective_id=0, has_side_effects=True, vmem_limit_bytes=52 * 1024 * 1024),
            name="pcg",
        )(*arrays)
        return pl.pallas_call(
            functools.partial(finish, chunks),
            out_shape=(jax.ShapeDtypeStruct(full, F32), jax.ShapeDtypeStruct(full, F32)),
            in_specs=[pl.BlockSpec(memory_space=pltpu.VMEM)] * 6,
            out_specs=(anywhere,) * 2,
            scratch_shapes=[vmem(*full), vmem(*full), dma((2, chunks))],
            compiler_params=pltpu.CompilerParams(vmem_limit_bytes=8 * 1024 * 1024),
            name="finish",
        )(*kept)

    spec = P("layer", "px", "py")
    return jax.shard_map(shards, mesh=mesh, in_specs=(spec,) * 6, out_specs=(spec, spec), check_vma=False)
```

time: 54.7 us -> 46.5 us (0.85)
  local copies, waits for them, and re-layouts: 4.63 us -> 0 us
  Pallas kernels: 49.3 us -> 45.7 us
    unnamed x4 -> x0, local copies, waits for them, and re-layouts: 4.63 us -> none
    pallas_call x1 -> x2, Pallas kernels: 49.3 us -> 45.7 us  [the longest x1 43.5 us: shards(): pl.pallas_call(functools.partial(kernel, sizes, chunks), out_shape=(vmem(...]
where the time goes in v1:
time: 46.5 us; the launch traced here: 46.4 us
  Pallas kernels  45.7 us (98%)
  between operations  0.64 us (1%)
    pallas_call x1, Pallas kernels, shards(): pl.pallas_call(functools.partial(kernel, sizes, chunks), out_shape=(vmem(...  43.5 us
    pallas_call x1, Pallas kernels, shards(): pl.pallas_call(functools.partial(finish, chunks), out_shape=(jax.ShapeDty...  2.22 us

profile of v1, /device:TPU:1, one launch (start us, length us, event | category | flops | bytes accessed | tf_op | source)
XLA Modules:
  0.0 46.4 jit_solution(9757476072475520424)
XLA Ops:
  0.6 43.5 %pcg.1 = (f32[4,128,1024]{2,1,0:T(8,128)S(1)}, f32[4,144,1024]{2,1,0:T(8,128)S(1)}, f32[4,144,1024]{2,1,0:T(8,128)S(1)}, f32[4,128,1024]{2,1,0:T(8,128)S(1)}, f3...) custom-call(f32[4,128,1024]{2,1,0:T(8,128)} %b_hbm.1, f32[4,128,1024]{2,1,0:T(8,128)} %r_hbm.1, ...), custom_call_target="tpu_custom_call" | custom-call | tf_op jit(solution)/shard_map/pcg/pallas_call | solution.py:481
  44.1 2.2 %finish.1 = (f32[4,128,1024]{2,1,0:T(8,128)}, f32[4,128,1024]{2,1,0:T(8,128)}) custom-call(f32[4,128,1024]{2,1,0:T(8,128)S(1)} %get-tuple-element.8.bb, f32[4,144,1024]{2,1,0:T(8,128)S(1)} %get-tuple-element.9.zb, f32[4,144,1024]{2,1,0:T(8,128)S(1)} %get-tuple-element.10.vb, f32[4,128,1024]{2,1,0:T(8,128)S(1)} %get-tuple-element.11.wb, ...), custom_call_target="tpu_custom_call" | custom-call | tf_op jit(solution)/shard_map/finish/pallas_call | solution.py:491
